TPU v7x, 32 devices: a whole 2x2x4 slice. The times are simulated.
32 devices in a mesh: dp: 16 (over z, y, x), mp: 2 (over core).
Axes of the slice: x: 2, y: 2, z: 4, core: 2. Of those that a mesh axis runs over, the one named last changes fastest.
Arguments:
- media: bfloat16 [256, 256, 1024], P('dp'), may hold values from -6 to 6
- slot_clip: int32 [256], P('dp'), may hold values from 0 to 15, as said below
- time_table: bfloat16 [144, 1024], replicated, may hold values from -6 to 6
- latents_init: float32 [64, 1024], replicated, may hold values from -6 to 6
- media_gain: float32 [2, 1024], replicated, may hold values from 0.5 to 1.5
- latent_gain: float32 [2, 1024], replicated, may hold values from 0.5 to 1.5
- final_gain: float32 [1024], replicated, may hold values from 0.5 to 1.5
- w_query: bfloat16 [2, 1024, 512], P(None, None, 'mp'), may hold values from -24 to 24
- w_key: bfloat16 [2, 1024, 512], P(None, None, 'mp'), may hold values from -0.1875 to 0.1875
- w_value: bfloat16 [2, 1024, 512], P(None, None, 'mp'), may hold values from -0.1875 to 0.1875
- w_out: bfloat16 [2, 512, 1024], P(None, 'mp'), may hold values from -0.5 to 0.5
Outputs:
- resampled: float32 [16, 64, 1024], P('dp')
Inputs may be any that keep to these rules, and one draw needn't show every extreme that they name: `slot_clip`: slot b lies on dp index b // 16, and its clip differs from that index by at most 4; differences of +4 and -4 both occur in every draw.
All inputs are finite; a program needn't handle non-finite values.
Results may differ from a plain program's by a relative error of at most 0.0085.
The roundings to bfloat16 on the way count: a program that leaves them out, or rounds other values in their place, can miss the bound.
Values may be sent and summed in bfloat16 or wider, within the bound.
A program may use at most 128 MiB of HBM per device.

v0:
```python
import jax
import jax.numpy as jnp
from jax import lax
from jax.sharding import PartitionSpec as P

HEAD_DIM = 64
LAYERS = 2
REACH = 4


epsilon = 1e-05
floor_score = -1e30


def carried_in(x, axis, combine, identity):
    count, index = (lax.axis_size(axis), lax.axis_index(axis))
    everything = lax.all_gather(x, axis)
    start = jnp.broadcast_to(jnp.asarray(identity, x.dtype), x.shape)

    def hop(k, before):
        reached = k < index
        new = combine(before, everything[k])
        return jnp.where(reached, new, before)

    return lax.fori_loop(0, count, hop, start)


def passed_along(value, axis, steps):
    count = lax.axis_size(axis)
    initial, last = (max(0, -steps), min(count, count - steps))
    return lax.ppermute(value, axis, [(source, source + steps) for source in range(initial, last)])


def normalize(values):
    mean = jnp.mean(values, axis=-1, keepdims=True)
    center = values - mean
    spread = jnp.mean(center * center, axis=-1, keepdims=True)
    return center / jnp.sqrt(spread + epsilon)


def weigh_acc(acc, weight):
    heads = weight.shape[-2]
    shaped = acc.reshape(acc.shape[:-1] + (heads, acc.shape[-1] // heads))
    scaled = shaped * jnp.swapaxes(weight, -1, -2)[..., None]
    return scaled.reshape(acc.shape)


def divide_heads(acc, total):
    heads = total.shape[-2]
    shaped = acc.reshape(acc.shape[:-1] + (heads, acc.shape[-1] // heads))
    scaled = shaped / jnp.swapaxes(total, -1, -2)[..., None]
    return scaled.reshape(acc.shape)


def block_stats(queries, keys, values):
    scores = jnp.einsum("bqhd,bkhd->bhqk", queries, keys, preferred_element_type=jnp.float32)
    top = jnp.max(scores, axis=-1)
    expo = jnp.exp(scores - top[..., None])
    total = jnp.sum(expo, axis=-1)
    weights = expo.astype(jnp.bfloat16)
    acc = jnp.einsum("bhqk,bkhd->bqhd", weights, values, preferred_element_type=jnp.float32)
    return (top, total, acc.reshape(acc.shape[0], acc.shape[1], -1))


def merge_pair(first, second):
    top_first = jnp.where(first[1] > 0.5, first[0], floor_score)
    top_second = jnp.where(second[1] > 0.5, second[0], floor_score)
    top = jnp.maximum(top_first, top_second)
    weight_first = jnp.exp(top_first - top)
    weight_second = jnp.exp(top_second - top)
    total = weight_first * first[1] + weight_second * second[1]
    acc = weigh_acc(first[2], weight_first) + weigh_acc(second[2], weight_second)
    return (top, total, acc)


def add_counts(earlier, later):
    return earlier + later


def local(
    media,
    slot_clip,
    time_table,
    latents_init,
    media_gain,
    latent_gain,
    final_gain,
    w_query,
    w_key,
    w_value,
    w_out,
):
    frames, patches, width = media.shape
    inner = w_query.shape[2]
    heads = inner // HEAD_DIM
    latent_count = latents_init.shape[0]
    span = 2 * REACH + 1
    here = lax.axis_index("dp")
    offsets = slot_clip - here + REACH
    same = slot_clip[:, None] == slot_clip[None, :]
    lower = jnp.arange(frames)[None, :] < jnp.arange(frames)[:, None]
    within = jnp.sum((same & lower).astype(jnp.int32), axis=1)
    clips = lax.axis_size("dp")
    member_clip = slot_clip[:, None] == jnp.arange(clips)[None, :]
    tally = jnp.sum(member_clip.astype(jnp.int32), axis=0)
    before = carried_in(tally, "dp", add_counts, jnp.zeros_like(tally))
    earlier = jnp.sum(jnp.where(member_clip, before[None, :], 0), axis=1)
    frame_index = earlier + within
    table_rows = time_table.shape[0]
    picker = (frame_index[:, None] == jnp.arange(table_rows)[None, :]).astype(jnp.bfloat16)
    stamp = jnp.dot(picker, time_table, preferred_element_type=jnp.float32)
    unit = normalize(media.astype(jnp.float32) + stamp[:, None, :])
    member = offsets[:, None] == jnp.arange(span)[None, :]
    share = member.astype(jnp.float32)
    state = latents_init
    for layer in range(LAYERS):
        normed = (unit * media_gain[layer]).astype(jnp.bfloat16).reshape(frames * patches, width)
        keys = jnp.dot(normed, w_key[layer], preferred_element_type=jnp.float32).astype(
            jnp.bfloat16
        )
        vals = jnp.dot(normed, w_value[layer], preferred_element_type=jnp.float32).astype(
            jnp.bfloat16
        )
        keys, vals = (
            keys.reshape(frames, patches, heads, HEAD_DIM),
            vals.reshape(frames, patches, heads, HEAD_DIM),
        )
        lat_norm = (normalize(state) * latent_gain[layer]).astype(jnp.bfloat16)
        query = (
            jnp.dot(lat_norm, w_query[layer], preferred_element_type=jnp.float32)
            * HEAD_DIM ** (-0.5)
        ).astype(jnp.bfloat16)
        self_keys = jnp.dot(lat_norm, w_key[layer], preferred_element_type=jnp.float32).astype(
            jnp.bfloat16
        )
        self_vals = jnp.dot(lat_norm, w_value[layer], preferred_element_type=jnp.float32).astype(
            jnp.bfloat16
        )
        window = query[None]
        length = 1
        while length < REACH + 1:
            needed = min(2 * length, REACH + 1)
            extra = needed - length
            received = passed_along(window[length - extra :], "dp", length)
            window = jnp.concatenate([received, window], axis=0)
            length = needed
        upward = query[None]
        length = 1
        while length < REACH + 1:
            needed = min(2 * length, REACH + 1)
            extra = needed - length
            arrived_up = passed_along(upward[:extra], "dp", -length)
            upward = jnp.concatenate([upward, arrived_up], axis=0)
            length = needed
        near_queries = jnp.concatenate([window, upward[1:]], axis=0)
        chosen = jnp.take(near_queries, offsets, axis=0).reshape(
            frames, latent_count, heads, HEAD_DIM
        )
        top, total, acc = block_stats(chosen, keys, vals)
        part_top = jnp.max(jnp.where(member[:, :, None, None], top[:, None], floor_score), axis=0)
        weight = jnp.exp(top - jnp.take(part_top, offsets, axis=0))
        part_total = jnp.sum(share[:, :, None, None] * (weight * total)[:, None], axis=0)
        part_acc = jnp.sum(share[:, :, None, None] * weigh_acc(acc, weight)[:, None], axis=0)
        shaped = (1, latent_count, heads, HEAD_DIM)
        own_top, own_total, own_acc = block_stats(
            query.reshape(shaped), self_keys.reshape(shaped), self_vals.reshape(shaped)
        )
        own = (own_top[0], own_total[0], own_acc[0])
        merged = own
        for slot in range(span):
            piece = (part_top[slot], part_total[slot], part_acc[slot])
            if slot != REACH:
                piece = passed_along((piece[0], piece[1], piece[2]), "dp", slot - REACH)
            merged = merge_pair(merged, piece)
        attn = divide_heads(merged[2], merged[1]).astype(jnp.bfloat16)
        change = jnp.dot(attn, w_out[layer], preferred_element_type=jnp.float32)
        state = state + lax.psum(change.astype(jnp.bfloat16), "mp").astype(jnp.float32)
    result = normalize(state) * final_gain
    return result[None]


def solution(mesh):
    return jax.shard_map(
        local,
        mesh=mesh,
        in_specs=(
            P("dp", None, None),
            P("dp"),
            P(),
            P(),
            P(),
            P(),
            P(),
            P(None, None, "mp"),
            P(None, None, "mp"),
            P(None, None, "mp"),
            P(None, "mp", None),
        ),
        out_specs=P("dp", None, None),
        check_vma=False,
    )
```

profile of v0, /device:TPU:0, one launch (start us, length us, event | category | flops | bytes accessed | tf_op | source)
XLA Modules:
  0.0 390.3 jit_solution(4535725415976579692)
XLA Ops:
  9.7 1.4 fusion.27
  13.7 5.5 %collective-permute-start.1 = (bf16[1,64,256]{2,1,0:T(8,128)(2,1)S(1)}, bf16[1,64,256]{2,1,0:T(8,128)(2,1)S(1)}, u32[]{:S(2)}, u32[]{:S(2)}) collective-permute-start(bf16[1,64,256]{2,1,0:T(8,128)(2,1)S(1)} %bitcast.340), channel_id=1, source_target_pairs={{0,2},{2,4},{4,6},{6,8},{8,10},{10,12},{12,14},{14,16},{16,18},{18... | collective-permute-start | bytes 98312 | tf_op jit(solution)/shard_map/ppermute | solution.py:31
  19.2 5.0 %collective-permute-start = (bf16[1,64,256]{2,1,0:T(8,128)(2,1)S(1)}, bf16[1,64,256]{2,1,0:T(8,128)(2,1)S(1)}, u32[]{:S(2)}, u32[]{:S(2)}) collective-permute-start(bf16[1,64,256]{2,1,0:T(8,128)(2,1)S(1)} %bitcast.341), channel_id=1, source_target_pairs={{0,8},{2,10},{4,12},{6,14},{8,16},{10,18},{12,20},{14,22},{16,24},... | collective-permute-start | bytes 98312 | tf_op jit(solution)/shard_map/ppermute | solution.py:31
  28.5 13.3 %all-reduce = s32[256]{0:T(256)S(1)} all-reduce(s32[256]{0:T(256)S(1)} %dynamic-update-slice), channel_id=2, replica_groups=mesh['dp'=16,'mp'=2] {'dp'}, use_global_device_ids=true, to_apply=%add | all-reduce | flops 256 | bytes 2048
  44.1 1.4 convolution_convert_fusion.8
  46.0 5.3 %fusion.1 = f32[16,256]{1,0:T(8,128)S(1)} fusion(bf16[16,256,1024]{2,1,0:T(8,128)(2,1)} %param.17, f32[16,1024]{1,0:T(8,128)S(1)} %fusion.100), kind=kLoop, calls=%fused_computation.11 | loop fusion | flops 12578816 | bytes 8470528 | tf_op jit(solution)/shard_map/reduce_sum | solution.py:35
  51.8 3.2 multiply_reduce_fusion
  55.1 12.0 %multiply_convert_fusion = (bf16[16,256,1024]{2,1,0:T(8,128)(2,1)}, bf16[16,256,1024]{2,1,0:T(8,128)(2,1)S(1)}) fusion(bf16[16,256,1024]{2,1,0:T(8,128)(2,1)S(1)} %copy-done.2, f32[1024]{0:T(1024)S(1)} %bitcast.350, f32[16,256]{1,0:T(8,128)S(1)} %add_sqrt_fusion, f32[16,256]{1,0:T(8,128)S(1)} %broadcast_multiply_fusion, f32[16,1024]{1,0:T(8,128)S(1)} %fusion.100, ...), kind=kLoop, calls=%fused_computation.6 | loop fusion | flops 33554432 | bytes 25272320 | tf_op jit(solution)/shard_map/convert_element_type | solution.py:117
  67.1 2.3 convolution_convert_fusion.2
  69.5 3.7 convolution_convert_fusion.3
  73.9 7.2 %convolution_convert_fusion = bf16[4096,256]{1,0:T(8,128)(2,1)} fusion(bf16[4096,1024]{1,0:T(8,128)(2,1)} %bitcast.330, bf16[2,1024,256]{2,1,0:T(8,128)(2,1)} %param.26), kind=kOutput, calls=%fused_computation.15 | convolution fusion | flops 2148532224 | bytes 11010048 | tf_op jit(solution)/shard_map/dot_general | solution.py:121
  81.3 7.1 %reshape.419 = bf16[16,256,4,64]{3,2,1,0:T(4,128)(2,1)} reshape(bf16[4096,256]{1,0:T(8,128)(2,1)} %convolution_convert_fusion.3) | data formatting | bytes 4194304 | tf_op jit(solution)/shard_map/reshape | solution.py:125
  88.4 3.2 reshape.420
  93.0 4.5 %collective-permute-start.2 = (bf16[2,64,256]{2,1,0:T(8,128)(2,1)S(1)}, bf16[2,64,256]{2,1,0:T(8,128)(2,1)S(1)}, u32[]{:S(2)}, u32[]{:S(2)}) collective-permute-start(bf16[2,64,256]{2,1,0:T(8,128)(2,1)S(1)} %get-tuple-element.179), channel_id=1, source_target_pairs={{0,4},{2,6},{4,8},{6,10},{8,12},{10,14},{12,16},{14,18},{16,20},{1... | collective-permute-start | bytes 196616 | tf_op jit(solution)/shard_map/ppermute | solution.py:31
  97.5 1.9 collective-permute-done.2
  100.6 5.7 %fusion.155 = (f32[16,4,64]{2,1,0:T(4,128)S(1)}, f32[16,4,64,256]{3,2,1,0:T(8,128)}) fusion(bf16[16,256,4,64]{3,2,1,0:T(4,128)(2,1)} %reshape.419, bf16[16,64,4,64]{3,2,1,0:T(4,128)(2,1)S(1)} %reshape.358), kind=kOutput, calls=%fused_computation.364 | convolution fusion | flops 135262208 | bytes 6832128 | tf_op jit(solution)/shard_map/bqhd,bkhd->bhqk/dot_general | solution.py:56
  107.7 3.3 fusion.12
  112.3 5.8 %collective-permute-start.28 = (f32[4,64]{1,0:T(4,128)S(1)}, f32[4,64]{1,0:T(4,128)S(1)}, u32[]{:S(2)}, u32[]{:S(2)}) collective-permute-start(f32[4,64]{1,0:T(4,128)S(1)} %get-tuple-element.197), channel_id=1, source_target_pairs={{0,8},{2,10},{4,12},{6,14},{8,16},{10,18},{12,20},{14,22},{16,24},... | collective-permute-start | bytes 3080 | tf_op jit(solution)/shard_map/ppermute | solution.py:31
  122.8 4.2 %bitcast_multiply_fusion.1 = f32[16,64,4,64]{1,3,2,0:T(8,128)S(1)} fusion(f32[16,4,64,256]{3,2,1,0:T(8,128)S(1)} %copy-done.4, f32[16,4,64]{2,1,0:T(4,128)S(1)} %get-tuple-element.242, bf16[16,256,4,64]{3,2,1,0:T(4,128)(2,1)} %reshape.420, f32[16,64,4]{1,2,0:T(4,128)S(1)} %get-tuple-element.174), kind=kOutput, calls=%fused_computation.34 | convolution fusion | flops 136577024 | bytes 7372800 | tf_op jit(solution)/shard_map/bhqk,bkhd->bqhd/dot_general | solution.py:61
  128.4 6.2 %collective-permute-start.25 = (f32[4,64]{1,0:T(4,128)}, f32[4,64]{1,0:T(4,128)S(1)}, u32[]{:S(2)}, u32[]{:S(2)}) collective-permute-start(f32[4,64]{1,0:T(4,128)} %get-tuple-element.198), channel_id=1, source_target_pairs={{0,6},{2,8},{4,10},{6,12},{8,14},{10,16},{12,18},{14,20},{16,22},{... | collective-permute-start | bytes 3080 | tf_op jit(solution)/shard_map/ppermute | solution.py:31
  134.6 4.9 %collective-permute-start.22 = (f32[4,64]{1,0:T(4,128)}, f32[4,64]{1,0:T(4,128)S(1)}, u32[]{:S(2)}, u32[]{:S(2)}) collective-permute-start(f32[4,64]{1,0:T(4,128)} %get-tuple-element.199), channel_id=1, source_target_pairs={{0,4},{2,6},{4,8},{6,10},{8,12},{10,14},{12,16},{14,18},{16,20},{1... | collective-permute-start | bytes 3080 | tf_op jit(solution)/shard_map/ppermute | solution.py:31
  142.2 3.1 collective-permute-done.13
  148.6 2.4 collective-permute-done.16
  151.0 4.3 %collective-permute-start.19 = (f32[4,64]{1,0:T(4,128)S(1)}, f32[4,64]{1,0:T(4,128)S(1)}, u32[]{:S(2)}, u32[]{:S(2)}) collective-permute-start(f32[4,64]{1,0:T(4,128)S(1)} %copy-done.16), channel_id=1, source_target_pairs={{0,2},{2,4},{4,6},{6,8},{8,10},{10,12},{12,14},{14,16},{16,18},{18... | collective-permute-start | bytes 3080 | tf_op jit(solution)/shard_map/ppermute | solution.py:31
  155.3 3.9 %collective-permute-start.18 = (f32[4,64]{1,0:T(4,128)S(1)}, f32[4,64]{1,0:T(4,128)S(1)}, u32[]{:S(2)}, u32[]{:S(2)}) collective-permute-start(f32[4,64]{1,0:T(4,128)S(1)} %get-tuple-element.208), channel_id=1, source_target_pairs={{0,2},{2,4},{4,6},{6,8},{8,10},{10,12},{12,14},{14,16},{16,18},{18... | collective-permute-start | bytes 3080 | tf_op jit(solution)/shard_map/ppermute | solution.py:31
  159.3 4.9 %collective-permute-start.27 = (f32[4,64]{1,0:T(4,128)}, f32[4,64]{1,0:T(4,128)S(1)}, u32[]{:S(2)}, u32[]{:S(2)}) collective-permute-start(f32[4,64]{1,0:T(4,128)} %get-tuple-element.205), channel_id=1, source_target_pairs={{0,8},{2,10},{4,12},{6,14},{8,16},{10,18},{12,20},{14,22},{16,24},... | collective-permute-start | bytes 3080 | tf_op jit(solution)/shard_map/ppermute | solution.py:31
  164.2 4.1 %collective-permute-start.21 = (f32[4,64]{1,0:T(4,128)S(1)}, f32[4,64]{1,0:T(4,128)S(1)}, u32[]{:S(2)}, u32[]{:S(2)}) collective-permute-start(f32[4,64]{1,0:T(4,128)S(1)} %get-tuple-element.207), channel_id=1, source_target_pairs={{0,4},{2,6},{4,8},{6,10},{8,12},{10,14},{12,16},{14,18},{16,20},{1... | collective-permute-start | bytes 3080 | tf_op jit(solution)/shard_map/ppermute | solution.py:31
  168.3 3.6 collective-permute-start.24
  173.3 4.5 %collective-permute-start.29 = (f32[64,256]{1,0:T(8,128)S(1)}, f32[64,256]{1,0:T(8,128)S(1)}, u32[]{:S(2)}, u32[]{:S(2)}) collective-permute-start(f32[64,256]{1,0:T(8,128)S(1)} %get-tuple-element.165), channel_id=1, source_target_pairs={{0,8},{2,10},{4,12},{6,14},{8,16},{10,18},{12,20},{14,22},{16,24},... | collective-permute-start | bytes 196616 | tf_op jit(solution)/shard_map/ppermute | solution.py:31
  177.8 5.1 %collective-permute-start.26 = (f32[64,256]{1,0:T(8,128)S(1)}, f32[64,256]{1,0:T(8,128)S(1)}, u32[]{:S(2)}, u32[]{:S(2)}) collective-permute-start(f32[64,256]{1,0:T(8,128)S(1)} %get-tuple-element.166), channel_id=1, source_target_pairs={{0,6},{2,8},{4,10},{6,12},{8,14},{10,16},{12,18},{14,20},{16,22},{... | collective-permute-start | bytes 196616 | tf_op jit(solution)/shard_map/ppermute | solution.py:31
  182.9 2.5 collective-permute-start.23
  185.5 3.6 collective-permute-start.20
  200.7 2.0 convolution_convert_fusion.5
  202.8 7.2 %convolution_convert_fusion.1 = bf16[4096,256]{1,0:T(8,128)(2,1)} fusion(bf16[4096,1024]{1,0:T(8,128)(2,1)} %bitcast.331, bf16[2,1024,256]{2,1,0:T(8,128)(2,1)} %param.25), kind=kOutput, calls=%fused_computation.16 | convolution fusion | flops 2148532224 | bytes 11010048 | tf_op jit(solution)/shard_map/dot_general | solution.py:118
  209.9 7.2 %reshape.421 = bf16[16,256,4,64]{3,2,1,0:T(4,128)(2,1)} reshape(bf16[4096,256]{1,0:T(8,128)(2,1)} %convolution_convert_fusion.1) | data formatting | bytes 4194304 | tf_op jit(solution)/shard_map/reshape | solution.py:125
  217.2 3.3 reshape.422
  220.5 3.3 all-reduce.4.cloned.1.call-done
  225.0 1.3 fusion.28
  230.5 4.5 %collective-permute-start.31 = (bf16[1,64,256]{2,1,0:T(8,128)(2,1)S(1)}, bf16[1,64,256]{2,1,0:T(8,128)(2,1)S(1)}, u32[]{:S(2)}, u32[]{:S(2)}) collective-permute-start(bf16[1,64,256]{2,1,0:T(8,128)(2,1)S(1)} %bitcast.345), channel_id=1, source_target_pairs={{0,2},{2,4},{4,6},{6,8},{8,10},{10,12},{12,14},{14,16},{16,18},{18... | collective-permute-start | bytes 98312 | tf_op jit(solution)/shard_map/ppermute | solution.py:31
  235.1 4.9 %collective-permute-start.30 = (bf16[1,64,256]{2,1,0:T(8,128)(2,1)S(1)}, bf16[1,64,256]{2,1,0:T(8,128)(2,1)S(1)}, u32[]{:S(2)}, u32[]{:S(2)}) collective-permute-start(bf16[1,64,256]{2,1,0:T(8,128)(2,1)S(1)} %bitcast.346), channel_id=1, source_target_pairs={{0,8},{2,10},{4,12},{6,14},{8,16},{10,18},{12,20},{14,22},{16,24},... | collective-permute-start | bytes 98312 | tf_op jit(solution)/shard_map/ppermute | solution.py:31
  242.1 4.5 %collective-permute-start.32 = (bf16[2,64,256]{2,1,0:T(8,128)(2,1)S(1)}, bf16[2,64,256]{2,1,0:T(8,128)(2,1)S(1)}, u32[]{:S(2)}, u32[]{:S(2)}) collective-permute-start(bf16[2,64,256]{2,1,0:T(8,128)(2,1)S(1)} %get-tuple-element.177), channel_id=1, source_target_pairs={{0,4},{2,6},{4,8},{6,10},{8,12},{10,14},{12,16},{14,18},{16,20},{1... | collective-permute-start | bytes 196616 | tf_op jit(solution)/shard_map/ppermute | solution.py:31
  246.7 1.9 collective-permute-done.32
  249.8 5.8 %fusion.157 = (f32[16,4,64]{2,1,0:T(4,128)S(1)}, f32[16,4,64,256]{3,2,1,0:T(8,128)}) fusion(bf16[16,256,4,64]{3,2,1,0:T(4,128)(2,1)} %reshape.421, bf16[16,64,4,64]{3,2,1,0:T(4,128)(2,1)S(1)} %reshape.365), kind=kOutput, calls=%fused_computation.366 | convolution fusion | flops 135262208 | bytes 6832128 | tf_op jit(solution)/shard_map/bqhd,bkhd->bhqk/dot_general | solution.py:56
  256.3 3.2 fusion.14
  260.9 6.9 %collective-permute-start.58 = (f32[4,64]{1,0:T(4,128)S(1)}, f32[4,64]{1,0:T(4,128)S(1)}, u32[]{:S(2)}, u32[]{:S(2)}) collective-permute-start(f32[4,64]{1,0:T(4,128)S(1)} %get-tuple-element.181), channel_id=1, source_target_pairs={{0,8},{2,10},{4,12},{6,14},{8,16},{10,18},{12,20},{14,22},{16,24},... | collective-permute-start | bytes 3080 | tf_op jit(solution)/shard_map/ppermute | solution.py:31
  272.0 4.0 %bitcast_multiply_fusion = f32[16,64,4,64]{1,3,2,0:T(8,128)S(1)} fusion(f32[16,4,64,256]{3,2,1,0:T(8,128)S(1)} %copy-done.3, f32[16,4,64]{2,1,0:T(4,128)S(1)} %get-tuple-element.246, bf16[16,256,4,64]{3,2,1,0:T(4,128)(2,1)} %reshape.422, f32[16,64,4]{1,2,0:T(4,128)S(1)} %get-tuple-element.172), kind=kOutput, calls=%fused_computation.33 | convolution fusion | flops 136577024 | bytes 7372800 | tf_op jit(solution)/shard_map/bhqk,bkhd->bqhd/dot_general | solution.py:61
  276.0 1.6 copy.95
  277.6 2.0 multiply_reduce_fusion.1
  280.3 6.1 %collective-permute-start.55 = (f32[4,64]{1,0:T(4,128)S(1)}, f32[4,64]{1,0:T(4,128)S(1)}, u32[]{:S(2)}, u32[]{:S(2)}) collective-permute-start(f32[4,64]{1,0:T(4,128)S(1)} %get-tuple-element.182), channel_id=1, source_target_pairs={{0,6},{2,8},{4,10},{6,12},{8,14},{10,16},{12,18},{14,20},{16,22},{... | collective-permute-start | bytes 3080 | tf_op jit(solution)/shard_map/ppermute | solution.py:31
  286.4 5.8 %collective-permute-start.52 = (f32[4,64]{1,0:T(4,128)S(1)}, f32[4,64]{1,0:T(4,128)S(1)}, u32[]{:S(2)}, u32[]{:S(2)}) collective-permute-start(f32[4,64]{1,0:T(4,128)S(1)} %get-tuple-element.183), channel_id=1, source_target_pairs={{0,4},{2,6},{4,8},{6,10},{8,12},{10,14},{12,16},{14,18},{16,20},{1... | collective-permute-start | bytes 3080 | tf_op jit(solution)/shard_map/ppermute | solution.py:31
  294.8 3.7 collective-permute-done.43
  301.8 2.2 collective-permute-done.46
  304.0 4.3 %collective-permute-start.49 = (f32[4,64]{1,0:T(4,128)S(1)}, f32[4,64]{1,0:T(4,128)S(1)}, u32[]{:S(2)}, u32[]{:S(2)}) collective-permute-start(f32[4,64]{1,0:T(4,128)S(1)} %get-tuple-element.184), channel_id=1, source_target_pairs={{0,2},{2,4},{4,6},{6,8},{8,10},{10,12},{12,14},{14,16},{16,18},{18... | collective-permute-start | bytes 3080 | tf_op jit(solution)/shard_map/ppermute | solution.py:31
  308.3 3.9 %collective-permute-start.48 = (f32[4,64]{1,0:T(4,128)S(1)}, f32[4,64]{1,0:T(4,128)S(1)}, u32[]{:S(2)}, u32[]{:S(2)}) collective-permute-start(f32[4,64]{1,0:T(4,128)S(1)} %get-tuple-element.192), channel_id=1, source_target_pairs={{0,2},{2,4},{4,6},{6,8},{8,10},{10,12},{12,14},{14,16},{16,18},{18... | collective-permute-start | bytes 3080 | tf_op jit(solution)/shard_map/ppermute | solution.py:31
  312.3 5.1 %collective-permute-start.57 = (f32[4,64]{1,0:T(4,128)S(1)}, f32[4,64]{1,0:T(4,128)S(1)}, u32[]{:S(2)}, u32[]{:S(2)}) collective-permute-start(f32[4,64]{1,0:T(4,128)S(1)} %get-tuple-element.189), channel_id=1, source_target_pairs={{0,8},{2,10},{4,12},{6,14},{8,16},{10,18},{12,20},{14,22},{16,24},... | collective-permute-start | bytes 3080 | tf_op jit(solution)/shard_map/ppermute | solution.py:31
  317.5 3.5 collective-permute-start.51
  321.0 3.4 collective-permute-start.54
  325.7 4.5 %collective-permute-start.59 = (f32[64,256]{1,0:T(8,128)S(1)}, f32[64,256]{1,0:T(8,128)S(1)}, u32[]{:S(2)}, u32[]{:S(2)}) collective-permute-start(f32[64,256]{1,0:T(8,128)S(1)} %get-tuple-element.157), channel_id=1, source_target_pairs={{0,8},{2,10},{4,12},{6,14},{8,16},{10,18},{12,20},{14,22},{16,24},... | collective-permute-start | bytes 196616 | tf_op jit(solution)/shard_map/ppermute | solution.py:31
  330.3 5.3 %collective-permute-start.56 = (f32[64,256]{1,0:T(8,128)S(1)}, f32[64,256]{1,0:T(8,128)S(1)}, u32[]{:S(2)}, u32[]{:S(2)}) collective-permute-start(f32[64,256]{1,0:T(8,128)S(1)} %get-tuple-element.158), channel_id=1, source_target_pairs={{0,6},{2,8},{4,10},{6,12},{8,14},{10,16},{12,18},{14,20},{16,22},{... | collective-permute-start | bytes 196616 | tf_op jit(solution)/shard_map/ppermute | solution.py:31
  335.6 2.5 collective-permute-start.53
  338.1 3.6 collective-permute-start.50
  355.4 2.1 convolution_convert_fusion.4
  357.5 21.6 %all-reduce.6.cloned.1.call-done = bf16[64,1024]{1,0:T(8,128)(2,1)} async-done(((bf16[64,1024]{1,0:T(8,128)(2,1)}), bf16[64,1024]{1,0:T(8,128)(2,1)}) %all-reduce.6.cloned.1.call-update) | async-done | bytes 131088 | tf_op jit(solution)/shard_map/psum | solution.py:177
  381.3 1.7 multiply_bitcast_fusion
  (367 shorter events, 82.1 us)
Async XLA Ops:
  6.5 217.2 %all-reduce.4.cloned.1.call-start = ((), (), s32[]{:S(2)}) async-start(), calls=%async_computation | async-start | bytes 262144 | tf_op jit(solution)/shard_map/psum | solution.py:177
  11.1 80.5 %collective-permute-start.3 = (bf16[1,64,256]{2,1,0:T(8,128)(2,1)S(1)}, bf16[1,64,256]{2,1,0:T(8,128)(2,1)S(1)}, u32[]{:S(2)}, u32[]{:S(2)}) collective-permute-start(bf16[1,64,256]{2,1,0:T(8,128)(2,1)S(1)} %bitcast.338), channel_id=1, source_target_pairs={{2,0},{4,2},{6,4},{8,6},{10,8},{12,10},{14,12},{16,14},{18,16},{20... | collective-permute-start | bytes 98312 | tf_op jit(solution)/shard_map/ppermute | solution.py:31
  12.4 87.1 %collective-permute-start.5 = (bf16[1,64,256]{2,1,0:T(8,128)(2,1)S(1)}, bf16[1,64,256]{2,1,0:T(8,128)(2,1)S(1)}, u32[]{:S(2)}, u32[]{:S(2)}) collective-permute-start(bf16[1,64,256]{2,1,0:T(8,128)(2,1)S(1)} %bitcast.339), channel_id=1, source_target_pairs={{8,0},{10,2},{12,4},{14,6},{16,8},{18,10},{20,12},{22,14},{24,16},... | collective-permute-start | bytes 98312 | tf_op jit(solution)/shard_map/ppermute | solution.py:31
  13.7 77.9 %collective-permute-start.1 = (bf16[1,64,256]{2,1,0:T(8,128)(2,1)S(1)}, bf16[1,64,256]{2,1,0:T(8,128)(2,1)S(1)}, u32[]{:S(2)}, u32[]{:S(2)}) collective-permute-start(bf16[1,64,256]{2,1,0:T(8,128)(2,1)S(1)} %bitcast.340), channel_id=1, source_target_pairs={{0,2},{2,4},{4,6},{6,8},{8,10},{10,12},{12,14},{14,16},{16,18},{18... | collective-permute-start | bytes 98312 | tf_op jit(solution)/shard_map/ppermute | solution.py:31
  19.2 78.3 %collective-permute-start = (bf16[1,64,256]{2,1,0:T(8,128)(2,1)S(1)}, bf16[1,64,256]{2,1,0:T(8,128)(2,1)S(1)}, u32[]{:S(2)}, u32[]{:S(2)}) collective-permute-start(bf16[1,64,256]{2,1,0:T(8,128)(2,1)S(1)} %bitcast.341), channel_id=1, source_target_pairs={{0,8},{2,10},{4,12},{6,14},{8,16},{10,18},{12,20},{14,22},{16,24},... | collective-permute-start | bytes 98312 | tf_op jit(solution)/shard_map/ppermute | solution.py:31
  91.7 7.8 %collective-permute-start.4 = (bf16[2,64,256]{2,1,0:T(8,128)(2,1)S(1)}, bf16[2,64,256]{2,1,0:T(8,128)(2,1)S(1)}, u32[]{:S(2)}, u32[]{:S(2)}) collective-permute-start(bf16[2,64,256]{2,1,0:T(8,128)(2,1)S(1)} %get-tuple-element.178), channel_id=1, source_target_pairs={{4,0},{6,2},{8,4},{10,6},{12,8},{14,10},{16,12},{18,14},{20,16},{2... | collective-permute-start | bytes 196616 | tf_op jit(solution)/shard_map/ppermute | solution.py:31
  93.0 6.4 %collective-permute-start.2 = (bf16[2,64,256]{2,1,0:T(8,128)(2,1)S(1)}, bf16[2,64,256]{2,1,0:T(8,128)(2,1)S(1)}, u32[]{:S(2)}, u32[]{:S(2)}) collective-permute-start(bf16[2,64,256]{2,1,0:T(8,128)(2,1)S(1)} %get-tuple-element.179), channel_id=1, source_target_pairs={{0,4},{2,6},{4,8},{6,10},{8,12},{10,14},{12,16},{14,18},{16,20},{1... | collective-permute-start | bytes 196616 | tf_op jit(solution)/shard_map/ppermute | solution.py:31
  111.0 17.5 %collective-permute-start.7 = (f32[4,64]{1,0:T(4,128)S(1)}, f32[4,64]{1,0:T(4,128)S(1)}, u32[]{:S(2)}, u32[]{:S(2)}) collective-permute-start(f32[4,64]{1,0:T(4,128)S(1)} %get-tuple-element.196), channel_id=1, source_target_pairs={{8,0},{10,2},{12,4},{14,6},{16,8},{18,10},{20,12},{22,14},{24,16},... | collective-permute-start | bytes 3080 | tf_op jit(solution)/shard_map/ppermute | solution.py:31
  112.3 70.7 %collective-permute-start.28 = (f32[4,64]{1,0:T(4,128)S(1)}, f32[4,64]{1,0:T(4,128)S(1)}, u32[]{:S(2)}, u32[]{:S(2)}) collective-permute-start(f32[4,64]{1,0:T(4,128)S(1)} %get-tuple-element.197), channel_id=1, source_target_pairs={{0,8},{2,10},{4,12},{6,14},{8,16},{10,18},{12,20},{14,22},{16,24},... | collective-permute-start | bytes 3080 | tf_op jit(solution)/shard_map/ppermute | solution.py:31
  118.1 16.6 %collective-permute-start.10 = (f32[4,64]{1,0:T(4,128)S(1)}, f32[4,64]{1,0:T(4,128)S(1)}, u32[]{:S(2)}, u32[]{:S(2)}) collective-permute-start(f32[4,64]{1,0:T(4,128)S(1)} %get-tuple-element.203), channel_id=1, source_target_pairs={{6,0},{8,2},{10,4},{12,6},{14,8},{16,10},{18,12},{20,14},{22,16},{... | collective-permute-start | bytes 3080 | tf_op jit(solution)/shard_map/ppermute | solution.py:31
  120.2 19.3 %collective-permute-start.6 = (f32[4,64]{1,0:T(4,128)S(1)}, f32[4,64]{1,0:T(4,128)S(1)}, u32[]{:S(2)}, u32[]{:S(2)}) collective-permute-start(f32[4,64]{1,0:T(4,128)S(1)} %get-tuple-element.204), channel_id=1, source_target_pairs={{8,0},{10,2},{12,4},{14,6},{16,8},{18,10},{20,12},{22,14},{24,16},... | collective-permute-start | bytes 3080 | tf_op jit(solution)/shard_map/ppermute | solution.py:31
  121.5 19.3 %collective-permute-start.9 = (f32[4,64]{1,0:T(4,128)S(1)}, f32[4,64]{1,0:T(4,128)S(1)}, u32[]{:S(2)}, u32[]{:S(2)}) collective-permute-start(f32[4,64]{1,0:T(4,128)S(1)} %get-tuple-element.211), channel_id=1, source_target_pairs={{6,0},{8,2},{10,4},{12,6},{14,8},{16,10},{18,12},{20,14},{22,16},{... | collective-permute-start | bytes 3080 | tf_op jit(solution)/shard_map/ppermute | solution.py:31
  128.4 72.4 %copy-start.8 = (bf16[2,256,1024]{2,1,0:T(8,128)(2,1)S(1)}, bf16[2,256,1024]{2,1,0:T(8,128)(2,1)}, u32[]{:S(2)}) copy-start(bf16[2,256,1024]{2,1,0:T(8,128)(2,1)} %param.27) | copy-start | bytes 3145732
  128.4 44.8 %collective-permute-start.25 = (f32[4,64]{1,0:T(4,128)}, f32[4,64]{1,0:T(4,128)S(1)}, u32[]{:S(2)}, u32[]{:S(2)}) collective-permute-start(f32[4,64]{1,0:T(4,128)} %get-tuple-element.198), channel_id=1, source_target_pairs={{0,6},{2,8},{4,10},{6,12},{8,14},{10,16},{12,18},{14,20},{16,22},{... | collective-permute-start | bytes 3080 | tf_op jit(solution)/shard_map/ppermute | solution.py:31
  134.6 33.7 %collective-permute-start.22 = (f32[4,64]{1,0:T(4,128)}, f32[4,64]{1,0:T(4,128)S(1)}, u32[]{:S(2)}, u32[]{:S(2)}) collective-permute-start(f32[4,64]{1,0:T(4,128)} %get-tuple-element.199), channel_id=1, source_target_pairs={{0,4},{2,6},{4,8},{6,10},{8,12},{10,14},{12,16},{14,18},{16,20},{1... | collective-permute-start | bytes 3080 | tf_op jit(solution)/shard_map/ppermute | solution.py:31
  139.5 5.8 %collective-permute-start.13 = (f32[4,64]{1,0:T(4,128)S(1)}, f32[4,64]{1,0:T(4,128)S(1)}, u32[]{:S(2)}, u32[]{:S(2)}) collective-permute-start(f32[4,64]{1,0:T(4,128)S(1)} %get-tuple-element.202), channel_id=1, source_target_pairs={{4,0},{6,2},{8,4},{10,6},{12,8},{14,10},{16,12},{18,14},{20,16},{2... | collective-permute-start | bytes 3080 | tf_op jit(solution)/shard_map/ppermute | solution.py:31
  140.8 6.4 %collective-permute-start.12 = (f32[4,64]{1,0:T(4,128)S(1)}, f32[4,64]{1,0:T(4,128)S(1)}, u32[]{:S(2)}, u32[]{:S(2)}) collective-permute-start(f32[4,64]{1,0:T(4,128)S(1)} %get-tuple-element.210), channel_id=1, source_target_pairs={{4,0},{6,2},{8,4},{10,6},{12,8},{14,10},{16,12},{18,14},{20,16},{2... | collective-permute-start | bytes 3080 | tf_op jit(solution)/shard_map/ppermute | solution.py:31
  145.3 5.7 %collective-permute-start.16 = (f32[4,64]{1,0:T(4,128)}, f32[4,64]{1,0:T(4,128)S(1)}, u32[]{:S(2)}, u32[]{:S(2)}) collective-permute-start(f32[4,64]{1,0:T(4,128)} %get-tuple-element.201), channel_id=1, source_target_pairs={{2,0},{4,2},{6,4},{8,6},{10,8},{12,10},{14,12},{16,14},{18,16},{20... | collective-permute-start | bytes 3080 | tf_op jit(solution)/shard_map/ppermute | solution.py:31
  147.2 8.0 %collective-permute-start.15 = (f32[4,64]{1,0:T(4,128)S(1)}, f32[4,64]{1,0:T(4,128)S(1)}, u32[]{:S(2)}, u32[]{:S(2)}) collective-permute-start(f32[4,64]{1,0:T(4,128)S(1)} %get-tuple-element.209), channel_id=1, source_target_pairs={{2,0},{4,2},{6,4},{8,6},{10,8},{12,10},{14,12},{16,14},{18,16},{20... | collective-permute-start | bytes 3080 | tf_op jit(solution)/shard_map/ppermute | solution.py:31
  151.0 8.3 %collective-permute-start.19 = (f32[4,64]{1,0:T(4,128)S(1)}, f32[4,64]{1,0:T(4,128)S(1)}, u32[]{:S(2)}, u32[]{:S(2)}) collective-permute-start(f32[4,64]{1,0:T(4,128)S(1)} %copy-done.16), channel_id=1, source_target_pairs={{0,2},{2,4},{4,6},{6,8},{8,10},{10,12},{12,14},{14,16},{16,18},{18... | collective-permute-start | bytes 3080 | tf_op jit(solution)/shard_map/ppermute | solution.py:31
  155.3 8.9 %collective-permute-start.18 = (f32[4,64]{1,0:T(4,128)S(1)}, f32[4,64]{1,0:T(4,128)S(1)}, u32[]{:S(2)}, u32[]{:S(2)}) collective-permute-start(f32[4,64]{1,0:T(4,128)S(1)} %get-tuple-element.208), channel_id=1, source_target_pairs={{0,2},{2,4},{4,6},{6,8},{8,10},{10,12},{12,14},{14,16},{16,18},{18... | collective-permute-start | bytes 3080 | tf_op jit(solution)/shard_map/ppermute | solution.py:31
  159.3 26.2 %collective-permute-start.27 = (f32[4,64]{1,0:T(4,128)}, f32[4,64]{1,0:T(4,128)S(1)}, u32[]{:S(2)}, u32[]{:S(2)}) collective-permute-start(f32[4,64]{1,0:T(4,128)} %get-tuple-element.205), channel_id=1, source_target_pairs={{0,8},{2,10},{4,12},{6,14},{8,16},{10,18},{12,20},{14,22},{16,24},... | collective-permute-start | bytes 3080 | tf_op jit(solution)/shard_map/ppermute | solution.py:31
  164.2 7.7 %collective-permute-start.21 = (f32[4,64]{1,0:T(4,128)S(1)}, f32[4,64]{1,0:T(4,128)S(1)}, u32[]{:S(2)}, u32[]{:S(2)}) collective-permute-start(f32[4,64]{1,0:T(4,128)S(1)} %get-tuple-element.207), channel_id=1, source_target_pairs={{0,4},{2,6},{4,8},{6,10},{8,12},{10,14},{12,16},{14,18},{16,20},{1... | collective-permute-start | bytes 3080 | tf_op jit(solution)/shard_map/ppermute | solution.py:31
  168.3 9.5 %collective-permute-start.24 = (f32[4,64]{1,0:T(4,128)S(1)}, f32[4,64]{1,0:T(4,128)S(1)}, u32[]{:S(2)}, u32[]{:S(2)}) collective-permute-start(f32[4,64]{1,0:T(4,128)S(1)} %get-tuple-element.206), channel_id=1, source_target_pairs={{0,6},{2,8},{4,10},{6,12},{8,14},{10,16},{12,18},{14,20},{16,22},{... | collective-permute-start | bytes 3080 | tf_op jit(solution)/shard_map/ppermute | solution.py:31
  171.9 17.2 %collective-permute-start.8 = (f32[64,256]{1,0:T(8,128)S(1)}, f32[64,256]{1,0:T(8,128)S(1)}, u32[]{:S(2)}, u32[]{:S(2)}) collective-permute-start(f32[64,256]{1,0:T(8,128)S(1)} %get-tuple-element.164), channel_id=1, source_target_pairs={{8,0},{10,2},{12,4},{14,6},{16,8},{18,10},{20,12},{22,14},{24,16},... | collective-permute-start | bytes 196616 | tf_op jit(solution)/shard_map/ppermute | solution.py:31
  173.3 17.1 %collective-permute-start.29 = (f32[64,256]{1,0:T(8,128)S(1)}, f32[64,256]{1,0:T(8,128)S(1)}, u32[]{:S(2)}, u32[]{:S(2)}) collective-permute-start(f32[64,256]{1,0:T(8,128)S(1)} %get-tuple-element.165), channel_id=1, source_target_pairs={{0,8},{2,10},{4,12},{6,14},{8,16},{10,18},{12,20},{14,22},{16,24},... | collective-permute-start | bytes 196616 | tf_op jit(solution)/shard_map/ppermute | solution.py:31
  177.8 13.9 %collective-permute-start.26 = (f32[64,256]{1,0:T(8,128)S(1)}, f32[64,256]{1,0:T(8,128)S(1)}, u32[]{:S(2)}, u32[]{:S(2)}) collective-permute-start(f32[64,256]{1,0:T(8,128)S(1)} %get-tuple-element.166), channel_id=1, source_target_pairs={{0,6},{2,8},{4,10},{6,12},{8,14},{10,16},{12,18},{14,20},{16,22},{... | collective-permute-start | bytes 196616 | tf_op jit(solution)/shard_map/ppermute | solution.py:31
  182.9 17.2 %collective-permute-start.23 = (f32[64,256]{1,0:T(8,128)S(1)}, f32[64,256]{1,0:T(8,128)}, u32[]{:S(2)}, u32[]{:S(2)}) collective-permute-start(f32[64,256]{1,0:T(8,128)S(1)} %get-tuple-element.167), channel_id=1, source_target_pairs={{0,4},{2,6},{4,8},{6,10},{8,12},{10,14},{12,16},{14,18},{16,20},{1... | collective-permute-start | bytes 196616 | tf_op jit(solution)/shard_map/ppermute | solution.py:31
  185.5 14.6 %collective-permute-start.20 = (f32[64,256]{1,0:T(8,128)S(1)}, f32[64,256]{1,0:T(8,128)}, u32[]{:S(2)}, u32[]{:S(2)}) collective-permute-start(f32[64,256]{1,0:T(8,128)S(1)} %get-tuple-element.168), channel_id=1, source_target_pairs={{0,2},{2,4},{4,6},{6,8},{8,10},{10,12},{12,14},{14,16},{16,18},{18... | collective-permute-start | bytes 196616 | tf_op jit(solution)/shard_map/ppermute | solution.py:31
  189.1 11.0 %collective-permute-start.17 = (f32[64,256]{1,0:T(8,128)S(1)}, f32[64,256]{1,0:T(8,128)}, u32[]{:S(2)}, u32[]{:S(2)}) collective-permute-start(f32[64,256]{1,0:T(8,128)S(1)} %get-tuple-element.169), channel_id=1, source_target_pairs={{2,0},{4,2},{6,4},{8,6},{10,8},{12,10},{14,12},{16,14},{18,16},{20... | collective-permute-start | bytes 196616 | tf_op jit(solution)/shard_map/ppermute | solution.py:31
  190.4 9.7 %collective-permute-start.14 = (f32[64,256]{1,0:T(8,128)S(1)}, f32[64,256]{1,0:T(8,128)}, u32[]{:S(2)}, u32[]{:S(2)}) collective-permute-start(f32[64,256]{1,0:T(8,128)S(1)} %get-tuple-element.170), channel_id=1, source_target_pairs={{4,0},{6,2},{8,4},{10,6},{12,8},{14,10},{16,12},{18,14},{20,16},{2... | collective-permute-start | bytes 196616 | tf_op jit(solution)/shard_map/ppermute | solution.py:31
  191.8 9.0 %collective-permute-start.11 = (f32[64,256]{1,0:T(8,128)S(1)}, f32[64,256]{1,0:T(8,128)}, u32[]{:S(2)}, u32[]{:S(2)}) collective-permute-start(f32[64,256]{1,0:T(8,128)S(1)} %get-tuple-element.171), channel_id=1, source_target_pairs={{6,0},{8,2},{10,4},{12,6},{14,8},{16,10},{18,12},{20,14},{22,16},{... | collective-permute-start | bytes 196616 | tf_op jit(solution)/shard_map/ppermute | solution.py:31
  202.7 176.4 %all-reduce.6.cloned.1.call-start = ((), (), s32[]{:S(2)}) async-start(), calls=%async_computation.1 | async-start | bytes 262144 | tf_op jit(solution)/shard_map/psum | solution.py:177
  227.9 12.9 %collective-permute-start.33 = (bf16[1,64,256]{2,1,0:T(8,128)(2,1)S(1)}, bf16[1,64,256]{2,1,0:T(8,128)(2,1)S(1)}, u32[]{:S(2)}, u32[]{:S(2)}) collective-permute-start(bf16[1,64,256]{2,1,0:T(8,128)(2,1)S(1)} %bitcast.343), channel_id=1, source_target_pairs={{2,0},{4,2},{6,4},{8,6},{10,8},{12,10},{14,12},{16,14},{18,16},{20... | collective-permute-start | bytes 98312 | tf_op jit(solution)/shard_map/ppermute | solution.py:31
  229.2 19.4 %collective-permute-start.35 = (bf16[1,64,256]{2,1,0:T(8,128)(2,1)S(1)}, bf16[1,64,256]{2,1,0:T(8,128)(2,1)S(1)}, u32[]{:S(2)}, u32[]{:S(2)}) collective-permute-start(bf16[1,64,256]{2,1,0:T(8,128)(2,1)S(1)} %bitcast.344), channel_id=1, source_target_pairs={{8,0},{10,2},{12,4},{14,6},{16,8},{18,10},{20,12},{22,14},{24,16},... | collective-permute-start | bytes 98312 | tf_op jit(solution)/shard_map/ppermute | solution.py:31
  230.5 10.3 %collective-permute-start.31 = (bf16[1,64,256]{2,1,0:T(8,128)(2,1)S(1)}, bf16[1,64,256]{2,1,0:T(8,128)(2,1)S(1)}, u32[]{:S(2)}, u32[]{:S(2)}) collective-permute-start(bf16[1,64,256]{2,1,0:T(8,128)(2,1)S(1)} %bitcast.345), channel_id=1, source_target_pairs={{0,2},{2,4},{4,6},{6,8},{8,10},{10,12},{12,14},{14,16},{16,18},{18... | collective-permute-start | bytes 98312 | tf_op jit(solution)/shard_map/ppermute | solution.py:31
  235.1 11.6 %collective-permute-start.30 = (bf16[1,64,256]{2,1,0:T(8,128)(2,1)S(1)}, bf16[1,64,256]{2,1,0:T(8,128)(2,1)S(1)}, u32[]{:S(2)}, u32[]{:S(2)}) collective-permute-start(bf16[1,64,256]{2,1,0:T(8,128)(2,1)S(1)} %bitcast.346), channel_id=1, source_target_pairs={{0,8},{2,10},{4,12},{6,14},{8,16},{10,18},{12,20},{14,22},{16,24},... | collective-permute-start | bytes 98312 | tf_op jit(solution)/shard_map/ppermute | solution.py:31
  240.8 7.8 %collective-permute-start.34 = (bf16[2,64,256]{2,1,0:T(8,128)(2,1)S(1)}, bf16[2,64,256]{2,1,0:T(8,128)(2,1)S(1)}, u32[]{:S(2)}, u32[]{:S(2)}) collective-permute-start(bf16[2,64,256]{2,1,0:T(8,128)(2,1)S(1)} %get-tuple-element.176), channel_id=1, source_target_pairs={{4,0},{6,2},{8,4},{10,6},{12,8},{14,10},{16,12},{18,14},{20,16},{2... | collective-permute-start | bytes 196616 | tf_op jit(solution)/shard_map/ppermute | solution.py:31
  242.1 6.4 %collective-permute-start.32 = (bf16[2,64,256]{2,1,0:T(8,128)(2,1)S(1)}, bf16[2,64,256]{2,1,0:T(8,128)(2,1)S(1)}, u32[]{:S(2)}, u32[]{:S(2)}) collective-permute-start(bf16[2,64,256]{2,1,0:T(8,128)(2,1)S(1)} %get-tuple-element.177), channel_id=1, source_target_pairs={{0,4},{2,6},{4,8},{6,10},{8,12},{10,14},{12,16},{14,18},{16,20},{1... | collective-permute-start | bytes 196616 | tf_op jit(solution)/shard_map/ppermute | solution.py:31
  259.6 20.7 %collective-permute-start.37 = (f32[4,64]{1,0:T(4,128)S(1)}, f32[4,64]{1,0:T(4,128)S(1)}, u32[]{:S(2)}, u32[]{:S(2)}) collective-permute-start(f32[4,64]{1,0:T(4,128)S(1)} %get-tuple-element.180), channel_id=1, source_target_pairs={{8,0},{10,2},{12,4},{14,6},{16,8},{18,10},{20,12},{22,14},{24,16},... | collective-permute-start | bytes 3080 | tf_op jit(solution)/shard_map/ppermute | solution.py:31
  260.9 74.7 %collective-permute-start.58 = (f32[4,64]{1,0:T(4,128)S(1)}, f32[4,64]{1,0:T(4,128)S(1)}, u32[]{:S(2)}, u32[]{:S(2)}) collective-permute-start(f32[4,64]{1,0:T(4,128)S(1)} %get-tuple-element.181), channel_id=1, source_target_pairs={{0,8},{2,10},{4,12},{6,14},{8,16},{10,18},{12,20},{14,22},{16,24},... | collective-permute-start | bytes 3080 | tf_op jit(solution)/shard_map/ppermute | solution.py:31
  267.8 18.6 %collective-permute-start.40 = (f32[4,64]{1,0:T(4,128)S(1)}, f32[4,64]{1,0:T(4,128)S(1)}, u32[]{:S(2)}, u32[]{:S(2)}) collective-permute-start(f32[4,64]{1,0:T(4,128)S(1)} %get-tuple-element.187), channel_id=1, source_target_pairs={{6,0},{8,2},{10,4},{12,6},{14,8},{16,10},{18,12},{20,14},{22,16},{... | collective-permute-start | bytes 3080 | tf_op jit(solution)/shard_map/ppermute | solution.py:31
  269.4 22.8 %collective-permute-start.36 = (f32[4,64]{1,0:T(4,128)S(1)}, f32[4,64]{1,0:T(4,128)S(1)}, u32[]{:S(2)}, u32[]{:S(2)}) collective-permute-start(f32[4,64]{1,0:T(4,128)S(1)} %get-tuple-element.188), channel_id=1, source_target_pairs={{8,0},{10,2},{12,4},{14,6},{16,8},{18,10},{20,12},{22,14},{24,16},... | collective-permute-start | bytes 3080 | tf_op jit(solution)/shard_map/ppermute | solution.py:31
  270.7 22.8 %collective-permute-start.39 = (f32[4,64]{1,0:T(4,128)S(1)}, f32[4,64]{1,0:T(4,128)S(1)}, u32[]{:S(2)}, u32[]{:S(2)}) collective-permute-start(f32[4,64]{1,0:T(4,128)S(1)} %get-tuple-element.195), channel_id=1, source_target_pairs={{6,0},{8,2},{10,4},{12,6},{14,8},{16,10},{18,12},{20,14},{22,16},{... | collective-permute-start | bytes 3080 | tf_op jit(solution)/shard_map/ppermute | solution.py:31
  279.6 75.8 %copy-start.9 = (bf16[2,256,1024]{2,1,0:T(8,128)(2,1)S(1)}, bf16[2,256,1024]{2,1,0:T(8,128)(2,1)}, u32[]{:S(2)}) copy-start(bf16[2,256,1024]{2,1,0:T(8,128)(2,1)} %param.27) | copy-start | bytes 3145732
  280.3 45.4 %collective-permute-start.55 = (f32[4,64]{1,0:T(4,128)S(1)}, f32[4,64]{1,0:T(4,128)S(1)}, u32[]{:S(2)}, u32[]{:S(2)}) collective-permute-start(f32[4,64]{1,0:T(4,128)S(1)} %get-tuple-element.182), channel_id=1, source_target_pairs={{0,6},{2,8},{4,10},{6,12},{8,14},{10,16},{12,18},{14,20},{16,22},{... | collective-permute-start | bytes 3080 | tf_op jit(solution)/shard_map/ppermute | solution.py:31
  286.4 34.6 %collective-permute-start.52 = (f32[4,64]{1,0:T(4,128)S(1)}, f32[4,64]{1,0:T(4,128)S(1)}, u32[]{:S(2)}, u32[]{:S(2)}) collective-permute-start(f32[4,64]{1,0:T(4,128)S(1)} %get-tuple-element.183), channel_id=1, source_target_pairs={{0,4},{2,6},{4,8},{6,10},{8,12},{10,14},{12,16},{14,18},{16,20},{1... | collective-permute-start | bytes 3080 | tf_op jit(solution)/shard_map/ppermute | solution.py:31
  292.2 6.4 %collective-permute-start.43 = (f32[4,64]{1,0:T(4,128)S(1)}, f32[4,64]{1,0:T(4,128)S(1)}, u32[]{:S(2)}, u32[]{:S(2)}) collective-permute-start(f32[4,64]{1,0:T(4,128)S(1)} %get-tuple-element.186), channel_id=1, source_target_pairs={{4,0},{6,2},{8,4},{10,6},{12,8},{14,10},{16,12},{18,14},{20,16},{2... | collective-permute-start | bytes 3080 | tf_op jit(solution)/shard_map/ppermute | solution.py:31
  293.5 7.0 %collective-permute-start.42 = (f32[4,64]{1,0:T(4,128)S(1)}, f32[4,64]{1,0:T(4,128)S(1)}, u32[]{:S(2)}, u32[]{:S(2)}) collective-permute-start(f32[4,64]{1,0:T(4,128)S(1)} %get-tuple-element.194), channel_id=1, source_target_pairs={{4,0},{6,2},{8,4},{10,6},{12,8},{14,10},{16,12},{18,14},{20,16},{2... | collective-permute-start | bytes 3080 | tf_op jit(solution)/shard_map/ppermute | solution.py:31
  298.6 5.5 %collective-permute-start.46 = (f32[4,64]{1,0:T(4,128)S(1)}, f32[4,64]{1,0:T(4,128)S(1)}, u32[]{:S(2)}, u32[]{:S(2)}) collective-permute-start(f32[4,64]{1,0:T(4,128)S(1)} %get-tuple-element.185), channel_id=1, source_target_pairs={{2,0},{4,2},{6,4},{8,6},{10,8},{12,10},{14,12},{16,14},{18,16},{20... | collective-permute-start | bytes 3080 | tf_op jit(solution)/shard_map/ppermute | solution.py:31
  300.5 7.8 %collective-permute-start.45 = (f32[4,64]{1,0:T(4,128)S(1)}, f32[4,64]{1,0:T(4,128)S(1)}, u32[]{:S(2)}, u32[]{:S(2)}) collective-permute-start(f32[4,64]{1,0:T(4,128)S(1)} %get-tuple-element.193), channel_id=1, source_target_pairs={{2,0},{4,2},{6,4},{8,6},{10,8},{12,10},{14,12},{16,14},{18,16},{20... | collective-permute-start | bytes 3080 | tf_op jit(solution)/shard_map/ppermute | solution.py:31
  304.0 8.3 %collective-permute-start.49 = (f32[4,64]{1,0:T(4,128)S(1)}, f32[4,64]{1,0:T(4,128)S(1)}, u32[]{:S(2)}, u32[]{:S(2)}) collective-permute-start(f32[4,64]{1,0:T(4,128)S(1)} %get-tuple-element.184), channel_id=1, source_target_pairs={{0,2},{2,4},{4,6},{6,8},{8,10},{10,12},{12,14},{14,16},{16,18},{18... | collective-permute-start | bytes 3080 | tf_op jit(solution)/shard_map/ppermute | solution.py:31
  308.3 9.1 %collective-permute-start.48 = (f32[4,64]{1,0:T(4,128)S(1)}, f32[4,64]{1,0:T(4,128)S(1)}, u32[]{:S(2)}, u32[]{:S(2)}) collective-permute-start(f32[4,64]{1,0:T(4,128)S(1)} %get-tuple-element.192), channel_id=1, source_target_pairs={{0,2},{2,4},{4,6},{6,8},{8,10},{10,12},{12,14},{14,16},{16,18},{18... | collective-permute-start | bytes 3080 | tf_op jit(solution)/shard_map/ppermute | solution.py:31
  312.3 25.8 %collective-permute-start.57 = (f32[4,64]{1,0:T(4,128)S(1)}, f32[4,64]{1,0:T(4,128)S(1)}, u32[]{:S(2)}, u32[]{:S(2)}) collective-permute-start(f32[4,64]{1,0:T(4,128)S(1)} %get-tuple-element.189), channel_id=1, source_target_pairs={{0,8},{2,10},{4,12},{6,14},{8,16},{10,18},{12,20},{14,22},{16,24},... | collective-permute-start | bytes 3080 | tf_op jit(solution)/shard_map/ppermute | solution.py:31
  317.5 6.9 %collective-permute-start.51 = (f32[4,64]{1,0:T(4,128)S(1)}, f32[4,64]{1,0:T(4,128)S(1)}, u32[]{:S(2)}, u32[]{:S(2)}) collective-permute-start(f32[4,64]{1,0:T(4,128)S(1)} %get-tuple-element.191), channel_id=1, source_target_pairs={{0,4},{2,6},{4,8},{6,10},{8,12},{10,14},{12,16},{14,18},{16,20},{1... | collective-permute-start | bytes 3080 | tf_op jit(solution)/shard_map/ppermute | solution.py:31
  321.0 9.3 %collective-permute-start.54 = (f32[4,64]{1,0:T(4,128)S(1)}, f32[4,64]{1,0:T(4,128)S(1)}, u32[]{:S(2)}, u32[]{:S(2)}) collective-permute-start(f32[4,64]{1,0:T(4,128)S(1)} %get-tuple-element.190), channel_id=1, source_target_pairs={{0,6},{2,8},{4,10},{6,12},{8,14},{10,16},{12,18},{14,20},{16,22},{... | collective-permute-start | bytes 3080 | tf_op jit(solution)/shard_map/ppermute | solution.py:31
  324.4 17.4 %collective-permute-start.38 = (f32[64,256]{1,0:T(8,128)S(1)}, f32[64,256]{1,0:T(8,128)S(1)}, u32[]{:S(2)}, u32[]{:S(2)}) collective-permute-start(f32[64,256]{1,0:T(8,128)S(1)} %get-tuple-element.156), channel_id=1, source_target_pairs={{8,0},{10,2},{12,4},{14,6},{16,8},{18,10},{20,12},{22,14},{24,16},... | collective-permute-start | bytes 196616 | tf_op jit(solution)/shard_map/ppermute | solution.py:31
  325.7 17.4 %collective-permute-start.59 = (f32[64,256]{1,0:T(8,128)S(1)}, f32[64,256]{1,0:T(8,128)S(1)}, u32[]{:S(2)}, u32[]{:S(2)}) collective-permute-start(f32[64,256]{1,0:T(8,128)S(1)} %get-tuple-element.157), channel_id=1, source_target_pairs={{0,8},{2,10},{4,12},{6,14},{8,16},{10,18},{12,20},{14,22},{16,24},... | collective-permute-start | bytes 196616 | tf_op jit(solution)/shard_map/ppermute | solution.py:31
  330.3 14.1 %collective-permute-start.56 = (f32[64,256]{1,0:T(8,128)S(1)}, f32[64,256]{1,0:T(8,128)S(1)}, u32[]{:S(2)}, u32[]{:S(2)}) collective-permute-start(f32[64,256]{1,0:T(8,128)S(1)} %get-tuple-element.158), channel_id=1, source_target_pairs={{0,6},{2,8},{4,10},{6,12},{8,14},{10,16},{12,18},{14,20},{16,22},{... | collective-permute-start | bytes 196616 | tf_op jit(solution)/shard_map/ppermute | solution.py:31
  335.6 19.8 %collective-permute-start.53 = (f32[64,256]{1,0:T(8,128)}, f32[64,256]{1,0:T(8,128)}, u32[]{:S(2)}, u32[]{:S(2)}) collective-permute-start(f32[64,256]{1,0:T(8,128)} %get-tuple-element.159), channel_id=1, source_target_pairs={{0,4},{2,6},{4,8},{6,10},{8,12},{10,14},{12,16},{14,18},{16,20},{1... | collective-permute-start | bytes 196616 | tf_op jit(solution)/shard_map/ppermute | solution.py:31
  338.1 17.2 %collective-permute-start.50 = (f32[64,256]{1,0:T(8,128)}, f32[64,256]{1,0:T(8,128)}, u32[]{:S(2)}, u32[]{:S(2)}) collective-permute-start(f32[64,256]{1,0:T(8,128)} %get-tuple-element.160), channel_id=1, source_target_pairs={{0,2},{2,4},{4,6},{6,8},{8,10},{10,12},{12,14},{14,16},{16,18},{18... | collective-permute-start | bytes 196616 | tf_op jit(solution)/shard_map/ppermute | solution.py:31
  341.8 13.6 %collective-permute-start.47 = (f32[64,256]{1,0:T(8,128)}, f32[64,256]{1,0:T(8,128)}, u32[]{:S(2)}, u32[]{:S(2)}) collective-permute-start(f32[64,256]{1,0:T(8,128)} %get-tuple-element.161), channel_id=1, source_target_pairs={{2,0},{4,2},{6,4},{8,6},{10,8},{12,10},{14,12},{16,14},{18,16},{20... | collective-permute-start | bytes 196616 | tf_op jit(solution)/shard_map/ppermute | solution.py:31
  343.1 12.3 %collective-permute-start.44 = (f32[64,256]{1,0:T(8,128)}, f32[64,256]{1,0:T(8,128)}, u32[]{:S(2)}, u32[]{:S(2)}) collective-permute-start(f32[64,256]{1,0:T(8,128)} %get-tuple-element.162), channel_id=1, source_target_pairs={{4,0},{6,2},{8,4},{10,6},{12,8},{14,10},{16,12},{18,14},{20,16},{2... | collective-permute-start | bytes 196616 | tf_op jit(solution)/shard_map/ppermute | solution.py:31
  344.4 11.0 %collective-permute-start.41 = (f32[64,256]{1,0:T(8,128)}, f32[64,256]{1,0:T(8,128)}, u32[]{:S(2)}, u32[]{:S(2)}) collective-permute-start(f32[64,256]{1,0:T(8,128)} %get-tuple-element.163), channel_id=1, source_target_pairs={{6,0},{8,2},{10,4},{12,6},{14,8},{16,10},{18,12},{20,14},{22,16},{... | collective-permute-start | bytes 196616 | tf_op jit(solution)/shard_map/ppermute | solution.py:31
  (19 other events, 302.0 us)
Sparse Core Ops, SparseCore 0:
  202.8 20.8 all-reduce.3
  357.6 21.4 all-reduce.5
where the time goes:
time: 398 us; the launch traced here: 390 us
  starting transfers between devices  176 us (44%)
  matrix products  50.9 us (13%)
  local copies, waits for them, and re-layouts  49.2 us (12%)
  waiting for transfers between devices  42.2 us (11%)
  other arithmetic  42 us (11%)
  between operations  16.3 us (4%)
  blocking collectives  13.3 us (3%)
    ppermute x60, starting transfers between devices, passed_along(): lax.ppermute(value, axis, [(source, source + steps) for source in range(i...  176 us
    psum x2, waiting for transfers between devices, local(): lax.psum(change.astype(jnp.bfloat16), 'mp').astype(jnp.float32)  24.9 us
    ppermute x60, waiting for transfers between devices, passed_along(): lax.ppermute(value, axis, [(source, source + steps) for source in range(i...  17.3 us
    reshape x2, local copies, waits for them, and re-layouts, local(): keys.reshape(frames, patches, heads, HEAD_DIM)  14.3 us
    unnamed x1, blocking collectives  13.3 us
    convert_element_type x1, other arithmetic, local(): (unit * media_gain[layer]).astype(jnp.bfloat16)  12 us
    dot_general x4, matrix products, block_stats(): jnp.einsum('bqhd,bkhd->bhqk', queries, keys, preferred_element_type=jnp.f...  11.9 us
    mul x72, local copies, waits for them, and re-layouts, weigh_acc(): scaled = shaped * jnp.swapaxes(weight, -1, -2)[..., None]  11.5 us
  transfers between devices with their start and end apart: 62, of which 11 were waited for; matrix products, arithmetic and copies ran while one was open for 26% of the time, Pallas kernels for 0%

commit v1 on v0

v1 whole, which is shorter than its diff:
```python
import functools

import jax
import jax.numpy as jnp
from jax import lax
from jax.experimental import pallas as pl
from jax.experimental.pallas import tpu as pltpu
from jax.sharding import PartitionSpec as P

HEAD_DIM = 64
LAYERS = 2
REACH = 4
SPAN = 2 * REACH + 1
epsilon = 1e-05
floor_score = -1e30
F32 = jnp.float32
BF16 = jnp.bfloat16


def normalize(values):
    mean = jnp.mean(values, axis=-1, keepdims=True)
    center = values - mean
    spread = jnp.mean(center * center, axis=-1, keepdims=True)
    return center * lax.rsqrt(spread + epsilon)


def dot(a, b):
    return jnp.dot(a, b, preferred_element_type=F32)


def dot_nt(a, b):
    return lax.dot_general(a, b, (((1,), (1,)), ((), ())), preferred_element_type=F32)


def spread_heads(query, heads):
    column = lax.broadcasted_iota(jnp.int32, query.shape, 1) // HEAD_DIM
    zero = jnp.zeros_like(query)
    return jnp.concatenate([jnp.where(column == h, query, zero) for h in range(heads)], axis=0)


def compact(column, heads, rows):
    lane = lax.broadcasted_iota(jnp.int32, (rows, 128), 1) % heads
    tile = jnp.broadcast_to(column[:rows], (rows, 128))
    for h in range(1, heads):
        tile = jnp.where(lane == h, column[h * rows : (h + 1) * rows], tile)
    return tile


def expand(tile, heads):
    rows = tile.shape[0]
    column = lax.broadcasted_iota(jnp.int32, (rows, heads * HEAD_DIM), 1) // HEAD_DIM
    wide = jnp.broadcast_to(tile[:, 0:1], column.shape)
    for h in range(1, heads):
        wide = jnp.where(column == h, tile[:, h : h + 1], wide)
    return wide


def block_stats(wide_query, keys, values, heads, rows):
    scores = dot_nt(wide_query, keys)
    top = jnp.max(scores, axis=-1, keepdims=True)
    expo = jnp.exp(scores - top)
    total = jnp.sum(expo, axis=-1, keepdims=True)
    product = dot(expo.astype(BF16), values)
    column = lax.broadcasted_iota(jnp.int32, (rows, product.shape[1]), 1) // HEAD_DIM
    acc = product[:rows]
    for h in range(1, heads):
        acc = jnp.where(column == h, product[h * rows : (h + 1) * rows], acc)
    return compact(top, heads, rows), compact(total, heads, rows), acc


def kernel(
    clips,
    split,
    clip_ref,
    media_hbm,
    table_hbm,
    latents_ref,
    media_gain_ref,
    latent_gain_ref,
    final_gain_ref,
    wq_hbm,
    wk_hbm,
    wv_hbm,
    wo_hbm,
    out_ref,
    media,
    table,
    wq,
    wkv,
    wo,
    normed,
    keyvals,
    state,
    stamp,
    row_out,
    row_in,
    count,
    tops,
    totals,
    accs,
    slot_top,
    own_tile,
    own_acc,
    part_acc,
    part_stat,
    got_acc,
    got_stat,
    query_out,
    query_in,
    wide,
    change_out,
    change_in,
    media_sem,
    weight_sem,
    row_sems,
    part_sems,
    query_sems,
    change_sems,
):
    me = lax.axis_index("dp")
    core = lax.axis_index("mp")
    frames, patches, width = media_hbm.shape
    rows = latents_ref.shape[0]
    inner = wq_hbm.shape[2]
    heads = inner // HEAD_DIM

    def load(index, source, target):
        return pltpu.make_async_copy(source, target, weight_sem.at[index])

    left, right = pl.ds(0, inner), pl.ds(inner, inner)
    loads = [
        load(0, wq_hbm.at[0], wq.at[0]),
        load(1, wk_hbm.at[0], wkv.at[0, :, left]),
        load(2, wv_hbm.at[0], wkv.at[0, :, right]),
        load(3, table_hbm, table),
        load(4, wk_hbm.at[1], wkv.at[1, :, left]),
        load(5, wv_hbm.at[1], wkv.at[1, :, right]),
        load(6, wo_hbm, wo),
        load(7, wq_hbm.at[1], wq.at[1]),
    ]

    def media_copy(f):
        return pltpu.make_async_copy(media_hbm.at[f], media.at[f], media_sem.at[f])

    for copy in loads[:4]:
        copy.start()

    @pl.loop(0, frames)
    def _(f):
        media_copy(f).start()

    for copy in loads[4:]:
        copy.start()

    barrier = pltpu.get_barrier_semaphore()
    for k in range(1, 2 * REACH + 1):
        for step in (k, -k):
            target = me + step

            @pl.when((target >= 0) & (target < clips))
            def _():
                pl.semaphore_signal(barrier, inc=1, device_id={"dp": target})

    pl.semaphore_signal(barrier, inc=1, device_id={"mp": 1 - core})

    lane = lax.broadcasted_iota(jnp.int32, (frames, 128), 1)
    sub = lax.broadcasted_iota(jnp.int32, (frames, 128), 0)
    own_row = jnp.full((frames, 128), -1, jnp.int32)
    own_col = jnp.full((frames, 128), -1, jnp.int32)
    for f in range(frames):
        own_row = jnp.where(lane == f, clip_ref[f], own_row)
        own_col = jnp.where(sub == f, clip_ref[f], own_col)
    row_out[...] = own_row[:8]
    count[...] = ((own_row == own_col) & (lane < sub)).astype(jnp.int32)

    below = jnp.minimum(me, 2 * REACH)
    above = jnp.minimum(clips - 1 - me, 2 * REACH)
    pl.semaphore_wait(barrier, below + above + 1)

    def row_copy(k):
        return pltpu.make_async_remote_copy(
            src_ref=row_out,
            dst_ref=row_in.at[k - 1],
            send_sem=row_sems.at[0, k - 1],
            recv_sem=row_sems.at[1, k - 1],
            device_id={"dp": me + k},
        )

    for k in range(1, 2 * REACH + 1):

        @pl.when(me + k < clips)
        def _():
            row_copy(k).start()

    def self_block(layer, lat_norm, query):
        both = dot(lat_norm, wkv[layer]).astype(BF16)
        top, total, acc = block_stats(
            spread_heads(query, heads), both[:, :inner], both[:, inner:], heads, rows
        )
        own_tile[0] = top
        own_tile[1] = total
        own_acc[...] = acc

    def lat_query(layer, values):
        lat_norm = (normalize(values) * latent_gain_ref[layer : layer + 1]).astype(BF16)
        query = (dot(lat_norm, wq[layer]) * HEAD_DIM**-0.5).astype(BF16)
        return lat_norm, query

    loads[0].wait()
    state[...] = latents_ref[...]
    lat_norm, query = lat_query(0, latents_ref[...])
    loads[1].wait()
    loads[2].wait()
    wide[REACH] = spread_heads(query, heads)
    self_block(0, lat_norm, query)

    for k in range(1, 2 * REACH + 1):

        @pl.when(me - k >= 0)
        def _():
            row_copy(k).wait_recv()
            count[...] += (row_in[k - 1, 0:1] == own_col).astype(jnp.int32)

    frame_index = jnp.sum(count[...].astype(F32), axis=1, keepdims=True).astype(jnp.int32)
    loads[3].wait()
    times = lax.broadcasted_iota(jnp.int32, (frames, table.shape[0]), 1)
    picker = (times == frame_index).astype(F32).astype(BF16)
    stamp[...] = dot(picker, table[...])

    chunk = 32

    @pl.loop(0, frames)
    def _(f):
        media_copy(f).wait()
        added = stamp[pl.ds(f, 1)]
        gain_0, gain_1 = media_gain_ref[0:1], media_gain_ref[1:2]
        for start in range(0, patches, chunk):
            piece = pl.ds(start, chunk)
            unit = normalize(media[f, piece].astype(F32) + added)
            normed[piece] = (unit * gain_0).astype(BF16)
            media[f, piece] = (unit * gain_1).astype(BF16)
        both = dot(normed[...], wkv[0]).astype(BF16)
        top, total, acc = block_stats(wide[REACH], both[:, :inner], both[:, inner:], heads, rows)
        tops[f] = top
        totals[f] = total
        accs[f] = acc

    def slot_of(f):
        return jnp.clip(clip_ref[f] - me + REACH, 0, SPAN - 1)

    def part_copies(layer, slot):
        target = me + slot - REACH
        return [
            pltpu.make_async_remote_copy(
                src_ref=source.at[layer, slot],
                dst_ref=into.at[layer, slot],
                send_sem=part_sems.at[layer, 0, which, slot],
                recv_sem=part_sems.at[layer, 1, which, slot],
                device_id={"dp": target},
            )
            for which, (source, into) in enumerate(((part_acc, got_acc), (part_stat, got_stat)))
        ]

    lane_q = lax.broadcasted_iota(jnp.int32, (rows, 128), 1)
    order = [slot for k in range(REACH, 0, -1) for slot in (REACH - k, REACH + k)] + [REACH]

    def reduce_slots(layer):
        @pl.loop(0, SPAN)
        def _(slot):
            best = jnp.full((rows, 128), floor_score, F32)
            for f in range(frames):
                bias = jnp.where(clip_ref[f] - me + REACH == slot, 0.0, floor_score)
                best = jnp.maximum(best, tops[f] + bias)
            slot_top[slot] = best

        @pl.loop(0, frames)
        def _(f):
            weight = jnp.exp(tops[f] - slot_top[slot_of(f)])
            totals[f] = totals[f] * weight
            accs[f] = accs[f] * expand(weight, heads)

        for slot in order:
            share = [
                jnp.where(clip_ref[f] - me + REACH == slot, 1.0, 0.0).astype(F32)
                for f in range(frames)
            ]
            total = jnp.zeros((rows, 128), F32)
            acc = jnp.zeros((rows, inner), F32)
            for f in range(frames):
                total = total + totals[f] * share[f]
                acc = acc + accs[f] * share[f]
            part_acc[layer, slot] = acc.astype(BF16)
            part_stat[layer, slot] = jnp.where((lane_q // heads) % 2 == 0, slot_top[slot], total)
            if slot != REACH:
                target = me + slot - REACH

                @pl.when((target >= 0) & (target < clips))
                def _():
                    for copy in part_copies(layer, slot):
                        copy.start()

    def merge(layer):
        for slot in order:
            if slot != REACH:
                source = me - (slot - REACH)
                here = (source >= 0) & (source < clips)

                @pl.when(here)
                def _():
                    for copy in part_copies(layer, slot):
                        copy.wait_recv()

                @pl.when(jnp.logical_not(here))
                def _():
                    got_acc[layer, slot] = jnp.zeros((rows, inner), BF16)
                    got_stat[layer, slot] = jnp.where(
                        (lane_q // heads) % 2 == 0, floor_score, 0.0
                    ).astype(F32)

        def stat(slot):
            return part_stat[layer, slot] if slot == REACH else got_stat[layer, slot]

        best = own_tile[0]
        for slot in range(SPAN):
            best = jnp.maximum(best, stat(slot))
        own_weight = jnp.exp(own_tile[0] - best)
        whole = own_weight * own_tile[1]
        weights = []
        for slot in range(SPAN):
            tile = stat(slot)
            weight = jnp.exp(tile - best)
            weights.append(weight)
            whole = whole + weight * pltpu.roll(tile, heads, 1)
        inverse = 1.0 / whole
        combined = own_acc[...] * expand(own_weight * inverse, heads)
        for slot in range(SPAN):
            acc = part_acc[layer, slot] if slot == REACH else got_acc[layer, slot]
            combined = combined + acc.astype(F32) * expand(weights[slot] * inverse, heads)
        return combined.astype(BF16)

    def change_copy(layer):
        return pltpu.make_async_remote_copy(
            src_ref=change_out.at[layer],
            dst_ref=change_in.at[layer],
            send_sem=change_sems.at[0, layer],
            recv_sem=change_sems.at[1, layer],
            device_id={"mp": 1 - core},
        )

    def update(layer):
        change_out[layer] = dot(merge(layer), wo[layer]).astype(BF16)
        change_copy(layer).start()
        change_copy(layer).wait_recv()
        return state[...] + (change_out[layer].astype(F32) + change_in[layer].astype(F32))

    def project(f):
        keyvals[f] = dot(media[f], wkv[1]).astype(BF16)

    reduce_slots(0)
    loads[4].wait()
    loads[5].wait()
    pl.loop(0, split)(project)
    loads[6].wait()
    state[...] = update(0)

    loads[7].wait()
    lat_norm, query = lat_query(1, state[...])
    query_out[...] = query

    def query_copy(slot):
        return pltpu.make_async_remote_copy(
            src_ref=query_out,
            dst_ref=query_in.at[slot],
            send_sem=query_sems.at[0, slot],
            recv_sem=query_sems.at[1, slot],
            device_id={"dp": me - (slot - REACH)},
        )

    for slot in order[:-1]:
        target = me - (slot - REACH)

        @pl.when((target >= 0) & (target < clips))
        def _():
            query_copy(slot).start()

    wide[REACH] = spread_heads(query, heads)
    self_block(1, lat_norm, query)
    pl.loop(split, frames)(project)

    for slot in order[:-1]:
        source = me + slot - REACH

        @pl.when((source >= 0) & (source < clips))
        def _():
            query_copy(slot).wait_recv()
            wide[slot] = spread_heads(query_in[slot], heads)

    @pl.loop(0, frames)
    def _(f):
        top, total, acc = block_stats(
            wide[slot_of(f)],
            keyvals[f, :, :inner],
            keyvals[f, :, inner:],
            heads,
            rows,
        )
        tops[f] = top
        totals[f] = total
        accs[f] = acc

    reduce_slots(1)
    out_ref[0] = normalize(update(1)) * final_gain_ref[...]

    for k in range(1, 2 * REACH + 1):

        @pl.when(me + k < clips)
        def _():
            row_copy(k).wait_send()

    for slot in order[:-1]:
        target = me + slot - REACH

        @pl.when((target >= 0) & (target < clips))
        def _():
            for layer in range(LAYERS):
                for copy in part_copies(layer, slot):
                    copy.wait_send()

        other = me - (slot - REACH)

        @pl.when((other >= 0) & (other < clips))
        def _():
            query_copy(slot).wait_send()

    for layer in range(LAYERS):
        change_copy(layer).wait_send()


def local(
    media,
    slot_clip,
    time_table,
    latents_init,
    media_gain,
    latent_gain,
    final_gain,
    w_query,
    w_key,
    w_value,
    w_out,
):
    frames, patches, width = media.shape
    inner = w_query.shape[2]
    heads = inner // HEAD_DIM
    rows = latents_init.shape[0]
    clips = lax.axis_size("dp")
    split = 10 * frames // 16
    vmem = pl.BlockSpec(memory_space=pltpu.VMEM)
    hbm = pl.BlockSpec(memory_space=pl.ANY)
    dma = pltpu.SemaphoreType.DMA
    scratch = [
        pltpu.VMEM((frames, patches, width), BF16),
        pltpu.VMEM(time_table.shape, BF16),
        pltpu.VMEM(w_query.shape, BF16),
        pltpu.VMEM((LAYERS, width, 2 * inner), BF16),
        pltpu.VMEM(w_out.shape, BF16),
        pltpu.VMEM((patches, width), BF16),
        pltpu.VMEM((frames, patches, 2 * inner), BF16),
        pltpu.VMEM((rows, width), F32),
        pltpu.VMEM((frames, width), F32),
        pltpu.VMEM((8, 128), jnp.int32),
        pltpu.VMEM((2 * REACH, 8, 128), jnp.int32),
        pltpu.VMEM((frames, 128), jnp.int32),
        pltpu.VMEM((frames, rows, 128), F32),
        pltpu.VMEM((frames, rows, 128), F32),
        pltpu.VMEM((frames, rows, inner), F32),
        pltpu.VMEM((SPAN, rows, 128), F32),
        pltpu.VMEM((2, rows, 128), F32),
        pltpu.VMEM((rows, inner), F32),
        pltpu.VMEM((LAYERS, SPAN, rows, inner), BF16),
        pltpu.VMEM((LAYERS, SPAN, rows, 128), F32),
        pltpu.VMEM((LAYERS, SPAN, rows, inner), BF16),
        pltpu.VMEM((LAYERS, SPAN, rows, 128), F32),
        pltpu.VMEM((rows, inner), BF16),
        pltpu.VMEM((SPAN, rows, inner), BF16),
        pltpu.VMEM((SPAN, heads * rows, inner), BF16),
        pltpu.VMEM((LAYERS, rows, width), BF16),
        pltpu.VMEM((LAYERS, rows, width), BF16),
        dma((frames,)),
        dma((8,)),
        dma((2, 2 * REACH)),
        dma((LAYERS, 2, 2, SPAN)),
        dma((2, SPAN)),
        dma((2, LAYERS)),
    ]
    return pl.pallas_call(
        functools.partial(kernel, clips, split),
        out_shape=jax.ShapeDtypeStruct((1, rows, width), F32),
        in_specs=[
            pl.BlockSpec(memory_space=pltpu.SMEM),
            hbm,
            hbm,
            vmem,
            vmem,
            vmem,
            vmem,
            hbm,
            hbm,
            hbm,
            hbm,
        ],
        out_specs=vmem,
        scratch_shapes=scratch,
        compiler_params=pltpu.CompilerParams(
            collective_id=0, has_side_effects=True, vmem_limit_bytes=60 * 1024 * 1024
        ),
    )(
        slot_clip,
        media,
        time_table,
        latents_init,
        media_gain,
        latent_gain,
        final_gain[None],
        w_query,
        w_key,
        w_value,
        w_out,
    )


def solution(mesh):
    return jax.shard_map(
        local,
        mesh=mesh,
        in_specs=(
            P("dp", None, None),
            P("dp"),
            P(),
            P(),
            P(),
            P(),
            P(),
            P(None, None, "mp"),
            P(None, None, "mp"),
            P(None, None, "mp"),
            P(None, "mp", None),
        ),
        out_specs=P("dp", None, None),
        check_vma=False,
    )
```

time: 398 us -> 67.1 us (0.17)
  the two profiles are of different devices: /device:TPU:0 before, /device:TPU:13 now
where the time goes in v1:
time: 67.1 us; the launch traced here: 67 us
  Pallas kernels  65.3 us (97%)
  local copies, waits for them, and re-layouts  1.67 us (2%)
    pallas_call x1, Pallas kernels, local(): pl.pallas_call(functools.partial(kernel, clips, split), out_shape=jax.Sha...  65.3 us
    unnamed x1, local copies, waits for them, and re-layouts  1.67 us

profile of v1, /device:TPU:13, one launch (start us, length us, event | category | flops | bytes accessed | tf_op | source)
XLA Modules:
  0.0 67.0 jit_solution(8757869945352984496)
XLA Ops:
  0.0 65.3 %shard_map.109 = f32[1,64,1024]{2,1,0:T(8,128)} custom-call(s32[16]{0:T(128)} %clip_ref.1, bf16[16,256,1024]{2,1,0:T(8,128)(2,1)} %media_hbm.1, bf16[144,1024]{1,0:T(8,128)(2,1)} %table_hbm.1, f32[64,1024]{1,0:T(8,128)} %latents_ref.1, f32[2,1024]{1,0:T(2,128)} %media_gain_ref.1, f32[2,1024]{1,0:T(2,128)} %latent_gain_ref.1, f32[1,1024]{1,0:T(1,128)} %bitcast.1, ...), custom_call_target="tpu_custom_call" | custom-call | tf_op jit(solution)/shard_map/pallas_call | solution.py:496
  65.3 1.7 %copy.13 = f32[1,64,1024]{2,1,0:T(8,128)} copy(f32[1,64,1024]{2,1,0:T(8,128)} %shard_map.109) | data formatting | bytes 524288

commit v2 on v1

--- a/solution.py
+++ b/solution.py
@@ -39,20 +39,26 @@
 
 
 def compact(column, heads, rows):
-    lane = lax.broadcasted_iota(jnp.int32, (rows, 128), 1) % heads
-    tile = jnp.broadcast_to(column[:rows], (rows, 128))
-    for h in range(1, heads):
-        tile = jnp.where(lane == h, column[h * rows : (h + 1) * rows], tile)
+    lane = lax.broadcasted_iota(jnp.int32, (8, 128), 1)
+    tile = jnp.zeros((8, 128), F32)
+    for g in range(rows // 8):
+        for h in range(heads):
+            here = (lane // (2 * heads) == g) & (lane % heads == h)
+            first = h * rows + 8 * g
+            tile = jnp.where(here, column[first : first + 8], tile)
     return tile
 
 
-def expand(tile, heads):
-    rows = tile.shape[0]
-    column = lax.broadcasted_iota(jnp.int32, (rows, heads * HEAD_DIM), 1) // HEAD_DIM
-    wide = jnp.broadcast_to(tile[:, 0:1], column.shape)
-    for h in range(1, heads):
-        wide = jnp.where(column == h, tile[:, h : h + 1], wide)
-    return wide
+def expand(tile, heads, rows):
+    column = lax.broadcasted_iota(jnp.int32, (8, heads * HEAD_DIM), 1) // HEAD_DIM
+    groups = []
+    for g in range(rows // 8):
+        first = 2 * heads * g
+        wide = jnp.broadcast_to(tile[:, first : first + 1], column.shape)
+        for h in range(1, heads):
+            wide = jnp.where(column == h, tile[:, first + h : first + h + 1], wide)
+        groups.append(wide)
+    return jnp.concatenate(groups, axis=0)
 
 
 def block_stats(wide_query, keys, values, heads, rows):
@@ -227,7 +233,7 @@
     picker = (times == frame_index).astype(F32).astype(BF16)
     stamp[...] = dot(picker, table[...])
 
-    chunk = 32
+    chunk = 16
 
     @pl.loop(0, frames)
     def _(f):
@@ -261,13 +267,13 @@
             for which, (source, into) in enumerate(((part_acc, got_acc), (part_stat, got_stat)))
         ]
 
-    lane_q = lax.broadcasted_iota(jnp.int32, (rows, 128), 1)
+    lane_q = lax.broadcasted_iota(jnp.int32, (8, 128), 1)
     order = [slot for k in range(REACH, 0, -1) for slot in (REACH - k, REACH + k)] + [REACH]
 
     def reduce_slots(layer):
         @pl.loop(0, SPAN)
         def _(slot):
-            best = jnp.full((rows, 128), floor_score, F32)
+            best = jnp.full((8, 128), floor_score, F32)
             for f in range(frames):
                 bias = jnp.where(clip_ref[f] - me + REACH == slot, 0.0, floor_score)
                 best = jnp.maximum(best, tops[f] + bias)
@@ -277,14 +283,14 @@
         def _(f):
             weight = jnp.exp(tops[f] - slot_top[slot_of(f)])
             totals[f] = totals[f] * weight
-            accs[f] = accs[f] * expand(weight, heads)
+            accs[f] = accs[f] * expand(weight, heads, rows)
 
         for slot in order:
             share = [
                 jnp.where(clip_ref[f] - me + REACH == slot, 1.0, 0.0).astype(F32)
                 for f in range(frames)
             ]
-            total = jnp.zeros((rows, 128), F32)
+            total = jnp.zeros((8, 128), F32)
             acc = jnp.zeros((rows, inner), F32)
             for f in range(frames):
                 total = total + totals[f] * share[f]
@@ -330,12 +336,12 @@
             tile = stat(slot)
             weight = jnp.exp(tile - best)
             weights.append(weight)
-            whole = whole + weight * pltpu.roll(tile, heads, 1)
+            whole = whole + weight * pltpu.roll(tile, 128 - heads, 1)
         inverse = 1.0 / whole
-        combined = own_acc[...] * expand(own_weight * inverse, heads)
+        combined = own_acc[...] * expand(own_weight * inverse, heads, rows)
         for slot in range(SPAN):
             acc = part_acc[layer, slot] if slot == REACH else got_acc[layer, slot]
-            combined = combined + acc.astype(F32) * expand(weights[slot] * inverse, heads)
+            combined = combined + acc.astype(F32) * expand(weights[slot] * inverse, heads, rows)
         return combined.astype(BF16)
 
     def change_copy(layer):
@@ -471,16 +477,16 @@
         pltpu.VMEM((8, 128), jnp.int32),
         pltpu.VMEM((2 * REACH, 8, 128), jnp.int32),
         pltpu.VMEM((frames, 128), jnp.int32),
-        pltpu.VMEM((frames, rows, 128), F32),
-        pltpu.VMEM((frames, rows, 128), F32),
+        pltpu.VMEM((frames, 8, 128), F32),
+        pltpu.VMEM((frames, 8, 128), F32),
         pltpu.VMEM((frames, rows, inner), F32),
-        pltpu.VMEM((SPAN, rows, 128), F32),
-        pltpu.VMEM((2, rows, 128), F32),
+        pltpu.VMEM((SPAN, 8, 128), F32),
+        pltpu.VMEM((2, 8, 128), F32),
         pltpu.VMEM((rows, inner), F32),
         pltpu.VMEM((LAYERS, SPAN, rows, inner), BF16),
-        pltpu.VMEM((LAYERS, SPAN, rows, 128), F32),
+        pltpu.VMEM((LAYERS, SPAN, 8, 128), F32),
         pltpu.VMEM((LAYERS, SPAN, rows, inner), BF16),
-        pltpu.VMEM((LAYERS, SPAN, rows, 128), F32),
+        pltpu.VMEM((LAYERS, SPAN, 8, 128), F32),
         pltpu.VMEM((rows, inner), BF16),
         pltpu.VMEM((SPAN, rows, inner), BF16),
         pltpu.VMEM((SPAN, heads * rows, inner), BF16),

time: 67.1 us -> 62.9 us (0.937); the launches traced: 67 us -> 62 us
  Pallas kernels: 65.3 us -> 60.3 us
    pallas_call x1, Pallas kernels: 65.3 us -> 60.3 us  [local(): pl.pallas_call(functools.partial(kernel, clips, split), out_shape=jax.Sha...]
where the time goes in v2:
time: 62.9 us; the launch traced here: 62 us
  Pallas kernels  60.3 us (96%)
  local copies, waits for them, and re-layouts  1.67 us (3%)
    pallas_call x1, Pallas kernels, local(): pl.pallas_call(functools.partial(kernel, clips, split), out_shape=jax.Sha...  60.3 us
    unnamed x1, local copies, waits for them, and re-layouts  1.67 us

profile of v2, /device:TPU:13, one launch (start us, length us, event | category | flops | bytes accessed | tf_op | source)
XLA Modules:
  0.0 62.0 jit_solution(7001974306889158779)
XLA Ops:
  0.0 60.3 %shard_map.109 = f32[1,64,1024]{2,1,0:T(8,128)} custom-call(s32[16]{0:T(128)} %clip_ref.1, bf16[16,256,1024]{2,1,0:T(8,128)(2,1)} %media_hbm.1, bf16[144,1024]{1,0:T(8,128)(2,1)} %table_hbm.1, f32[64,1024]{1,0:T(8,128)} %latents_ref.1, f32[2,1024]{1,0:T(2,128)} %media_gain_ref.1, f32[2,1024]{1,0:T(2,128)} %latent_gain_ref.1, f32[1,1024]{1,0:T(1,128)} %bitcast.1, ...), custom_call_target="tpu_custom_call" | custom-call | tf_op jit(solution)/shard_map/pallas_call | solution.py:502
  60.3 1.7 %copy.13 = f32[1,64,1024]{2,1,0:T(8,128)} copy(f32[1,64,1024]{2,1,0:T(8,128)} %shard_map.109) | data formatting | bytes 524288
